TPU v7x, 32 devices: a whole 2x2x4 slice. The times are simulated.
32 devices in a mesh: freq: 4 (over y, x), pts: 8 (over z, core).
Axes of the slice: x: 2, y: 2, z: 4, core: 2. Of those that a mesh axis runs over, the one named last changes fastest.
Arguments:
- data: float32 [2, 32, 64, 3, 8192], P(None, 'freq', None, None, 'pts'), may hold values from -180 to 180
- quad_weight: float32 [8192], P('pts'), may hold values from 0.2 to 5
- basis: float32 [2, 32, 64, 8], P(None, 'freq'), may hold values from -6 to 6
Outputs:
- basis_out: float32 [2, 32, 64, 8], P(None, 'freq')
- spectrum: float32 [32, 8], P('freq')
- modes: float32 [2, 32, 8, 3, 8192], P(None, 'freq', None, None, 'pts')
All inputs are finite; a program needn't handle non-finite values.
Results may differ from a plain program's by a relative error of at most 0.0001.
Values sent between devices are 32-bit elements; how exact they have to be, the bound alone decides.
A program may use at most 128 MiB of HBM per device.

v0:
```python
import functools

import jax
import jax.numpy as jnp
from jax import lax
from jax.experimental import pallas as pl
from jax.experimental.pallas import tpu as pltpu
from jax.sharding import PartitionSpec as P

ITERS = 4
MESH = pl.DeviceIdType.MESH


def spod_kernel(
    scaling,
    freqs,
    peers,
    groups,
    data_ref,
    weight_ref,
    basis_ref,
    basis_out_ref,
    spectrum_ref,
    modes_ref,
    buf,
    split,
    stage,
    gram_out,
    gram_in,
    trace_out,
    trace_in,
    message,
    load_sem,
    store_sem,
    gram_send,
    gram_recv,
    trace_send,
    trace_recv,
    msg_send,
    msg_recv,
):
    comps, blocks, points = buf.shape[2], buf.shape[3], buf.shape[4]
    rank = basis_ref.shape[2]
    wide = 2 * blocks
    stride = peers // freqs
    me = lax.axis_index("pts")
    row = lax.axis_index("freq")
    mine = me // stride
    is_owner = lax.rem(me, stride) == 0

    def load(f):
        return pltpu.make_async_copy(data_ref.at[:, f], buf.at[f], load_sem.at[f])

    def order(i):
        return lax.rem(mine + 1 + i, freqs)

    for i in range(freqs):
        load(order(i)).start()

    barrier = pltpu.get_barrier_semaphore()
    for step in range(1, peers):
        pl.semaphore_signal(
            barrier, inc=1, device_id={"pts": lax.rem(me + step, peers)}, device_id_type=MESH
        )
    for step in range(1, groups):
        pl.semaphore_signal(
            barrier, inc=1, device_id={"freq": lax.rem(row + step, groups)}, device_id_type=MESH
        )

    root = jnp.sqrt(weight_ref[...])
    inverse = (1.0 / blocks) / root
    lanes = lax.broadcasted_iota(jnp.int32, (1, wide), 1)
    low_minus = jnp.where(lanes < blocks, -1.0, 1.0).astype(jnp.float32)
    high_minus = -low_minus

    def local_gram(f):
        load(f).wait()
        total = jnp.zeros((wide, 2 * wide), jnp.float32)
        for c in range(comps):
            for part in range(2):
                value = buf[f, part, c] * root
                high = value.astype(jnp.bfloat16)
                rest = (value - high.astype(jnp.float32)).astype(jnp.bfloat16)
                split[f, c, part * blocks : (part + 1) * blocks] = high
                split[f, c, wide + part * blocks : wide + (part + 1) * blocks] = rest
            total = total + lax.dot_general(
                split[f, c, :wide],
                split[f, c],
                (((1,), (1,)), ((), ())),
                preferred_element_type=jnp.float32,
            )
        half = 0.5 * total[:, :wide] + total[:, wide:]
        return half[:blocks] + high_minus * pltpu.roll(half[blocks:], blocks, 1)

    def gram_copy(f):
        return pltpu.make_async_remote_copy(
            src_ref=gram_out.at[f],
            dst_ref=gram_in.at[me],
            send_sem=gram_send.at[f],
            recv_sem=gram_recv.at[me],
            device_id={"pts": f * stride},
            device_id_type=MESH,
        )

    first = order(0)
    gram_out[first] = local_gram(first)
    pl.semaphore_wait(barrier, peers - 1 + groups - 1)
    gram_copy(first).start()

    def middle(i, carry):
        f = order(i)
        gram_out[f] = local_gram(f)
        gram_copy(f).start()
        return carry

    lax.fori_loop(1, freqs - 1, middle, 0)
    gram_out[mine] = local_gram(mine)

    if stride > 1:

        @pl.when(jnp.logical_not(is_owner))
        def _():
            gram_copy(mine).start()

    def trace_copy(step):
        return pltpu.make_async_remote_copy(
            src_ref=trace_out,
            dst_ref=trace_in.at[row],
            send_sem=trace_send.at[step],
            recv_sem=trace_recv.at[row],
            device_id={"freq": lax.rem(row + step, groups)},
            device_id_type=MESH,
        )

    def msg_copy(step):
        return pltpu.make_async_remote_copy(
            src_ref=message.at[mine],
            dst_ref=message.at[mine],
            send_sem=msg_send.at[step],
            recv_sem=msg_recv.at[mine],
            device_id={"pts": lax.rem(me + step, peers)},
            device_id_type=MESH,
        )

    @pl.when(is_owner)
    def _():
        def gather(step, total):
            source = lax.rem(me + step, peers)
            pltpu.make_async_copy(gram_in.at[source], gram_in.at[source], gram_recv.at[source]).wait()
            return total + gram_in[source]

        total = lax.fori_loop(1, peers, gather, gram_out[mine]) * scaling
        double = jnp.concatenate([high_minus * total, pltpu.roll(total, blocks, 1)], axis=0)
        matrix = double + double.T
        rows_at = lax.broadcasted_iota(jnp.int32, (wide, wide), 0)
        cols_at = lax.broadcasted_iota(jnp.int32, (wide, wide), 1)
        diagonal = jnp.where(rows_at == cols_at, matrix, 0.0)
        trace = 0.5 * jnp.sum(jnp.sum(diagonal, axis=0, keepdims=True), axis=1, keepdims=True)
        trace_out[...] = jnp.broadcast_to(trace, trace_out.shape)
        for step in range(1, groups):
            trace_copy(step).start()

        def apply(vec):
            return jnp.dot(
                vec, matrix, precision=lax.Precision.HIGHEST, preferred_element_type=jnp.float32
            )

        which = lax.broadcasted_iota(jnp.int32, (rank, wide), 0)

        def step_body(step, vec):
            z = apply(vec)
            turned = low_minus * pltpu.roll(z, blocks, 1)
            for j in range(rank):
                base = z[j : j + 1]
                base_turned = turned[j : j + 1]
                along = jnp.sum(z * base, axis=1, keepdims=True) * (1.0 / blocks)
                across = jnp.sum(z * base_turned, axis=1, keepdims=True) * (1.0 / blocks)
                factor = lax.rsqrt(along[j : j + 1] + 1e-06)
                unit = base * factor
                unit_turned = base_turned * factor
                along = along * factor
                across = across * factor
                z_next = z - (along * unit + across * unit_turned)
                turned_next = turned - (along * unit_turned - across * unit)
                z = jnp.where(which > j, z_next, jnp.where(which == j, unit, z))
                turned = jnp.where(which > j, turned_next, turned)
            return z

        start = jnp.concatenate([basis_ref[0, mine], basis_ref[1, mine]], axis=1)
        vec = lax.fori_loop(0, ITERS, step_body, start)
        energy = jnp.sum(vec * apply(vec), axis=1, keepdims=True) * (1.0 / blocks)
        columns = lax.broadcasted_iota(jnp.int32, (rank, wide), 1)
        energy_row = jnp.sum(jnp.where(which == columns, energy, 0.0), axis=0, keepdims=True)

        group_trace = trace_out[...]
        for step in range(1, groups):
            source = lax.rem(row + step, groups)
            pltpu.make_async_copy(trace_in.at[source], trace_in.at[source], trace_recv.at[source]).wait()
            group_trace = group_trace + trace_in[source]
        message[mine, 0:rank] = vec
        message[mine, rank : rank + 8] = jnp.where(
            lax.broadcasted_iota(jnp.int32, (8, wide), 0) == 0, energy_row, group_trace
        )
        for step in range(1, peers):
            msg_copy(step).start()

    def project(f):
        vec = message[f, 0:rank]
        left = jnp.concatenate([high_minus * vec, pltpu.roll(vec, blocks, 1)], axis=0)
        high = left.astype(jnp.bfloat16)
        rest = (left - high.astype(jnp.float32)).astype(jnp.bfloat16)
        both = jnp.concatenate([high, high], axis=1)
        tail = jnp.concatenate([rest, jnp.zeros_like(rest)], axis=1)
        left = jnp.concatenate([both, tail], axis=0)
        for c in range(comps):
            out = jnp.dot(left, split[f, c], preferred_element_type=jnp.float32)
            out = (out[: 2 * rank] + out[2 * rank :]) * inverse
            stage[f, 0, c] = out[:rank]
            stage[f, 1, c] = out[rank:]
        basis_out_ref[0, f] = vec[:, :blocks]
        basis_out_ref[1, f] = pltpu.roll(vec, blocks, 1)[:, :blocks]
        store(f).start()

    def store(f):
        return pltpu.make_async_copy(stage.at[f], modes_ref.at[:, f], store_sem.at[f])

    def arrive(f):
        pltpu.make_async_copy(message.at[f], message.at[f], msg_recv.at[f]).wait()

    if stride > 1:

        @pl.when(jnp.logical_not(is_owner))
        def _():
            arrive(mine)

    project(mine)

    def others(i, carry):
        f = lax.rem(mine + freqs - i, freqs)
        arrive(f)
        project(f)
        return carry

    lax.fori_loop(1, freqs, others, 0)

    energies = []
    overall = jnp.zeros((1, wide), jnp.float32)
    for f in range(freqs):
        energies.append(message[f, rank : rank + 1])
        overall = overall + message[f, rank + 1 : rank + 2]
    count = freqs * groups * blocks
    spectrum_ref[...] = (jnp.concatenate(energies, axis=0) * count / overall)[:, :rank]

    def finish(i, carry):
        gram_copy(order(i)).wait_send()
        return carry

    lax.fori_loop(0, freqs - 1, finish, 0)
    if stride > 1:

        @pl.when(jnp.logical_not(is_owner))
        def _():
            gram_copy(mine).wait_send()

    @pl.when(is_owner)
    def _():
        for step in range(1, groups):
            trace_copy(step).wait_send()
        for step in range(1, peers):
            msg_copy(step).wait_send()

    for f in range(freqs):
        store(f).wait()


def per_device(peers, groups, data, quad_weight, basis):
    _, freqs, blocks, comps, points = data.shape
    rank = basis.shape[-1]
    assert peers % freqs == 0 and freqs > 2
    scaling = 1.0 / (comps * points * peers)
    wide = 2 * blocks
    vmem = pl.BlockSpec(memory_space=pltpu.VMEM)
    anywhere = pl.BlockSpec(memory_space=pl.ANY)
    f32 = jnp.float32
    basis_t, spectrum, modes_t = pl.pallas_call(
        functools.partial(spod_kernel, scaling, freqs, peers, groups),
        out_shape=(
            jax.ShapeDtypeStruct((2, freqs, rank, blocks), f32),
            jax.ShapeDtypeStruct((freqs, rank), f32),
            jax.ShapeDtypeStruct((2, freqs, comps, rank, points), f32),
        ),
        in_specs=[anywhere, vmem, vmem],
        out_specs=(vmem, vmem, anywhere),
        scratch_shapes=[
            pltpu.VMEM((freqs, 2, comps, blocks, points), f32),
            pltpu.VMEM((freqs, comps, 2 * wide, points), jnp.bfloat16),
            pltpu.VMEM((freqs, 2, comps, rank, points), f32),
            pltpu.VMEM((freqs, blocks, wide), f32),
            pltpu.VMEM((peers, blocks, wide), f32),
            pltpu.VMEM((8, wide), f32),
            pltpu.VMEM((groups, 8, wide), f32),
            pltpu.VMEM((freqs, rank + 8, wide), f32),
            pltpu.SemaphoreType.DMA((freqs,)),
            pltpu.SemaphoreType.DMA((freqs,)),
            pltpu.SemaphoreType.DMA((freqs,)),
            pltpu.SemaphoreType.DMA((peers,)),
            pltpu.SemaphoreType.DMA((groups,)),
            pltpu.SemaphoreType.DMA((groups,)),
            pltpu.SemaphoreType.DMA((peers,)),
            pltpu.SemaphoreType.DMA((freqs,)),
        ],
        compiler_params=pltpu.CompilerParams(
            collective_id=0, has_side_effects=True, vmem_limit_bytes=60 * 1024 * 1024
        ),
        name="spod",
    )(
        data.transpose(0, 1, 3, 2, 4),
        quad_weight.reshape(1, points),
        basis.transpose(0, 1, 3, 2),
    )
    return (
        basis_t.transpose(0, 1, 3, 2),
        spectrum,
        modes_t.transpose(0, 1, 3, 2, 4),
    )


def solution(mesh):
    in_specs = (P(None, "freq", None, None, "pts"), P("pts"), P(None, "freq", None, None))
    out_specs = (P(None, "freq", None, None), P("freq", None), P(None, "freq", None, None, "pts"))
    body = functools.partial(per_device, mesh.shape["pts"], mesh.shape["freq"])
    return jax.shard_map(
        body, mesh=mesh, in_specs=in_specs, out_specs=out_specs, check_vma=False
    )
```

profile of v0, /device:TPU:0, one launch (start us, length us, event | category | flops | bytes accessed | tf_op | source)
XLA Modules:
  0.0 32.3 jit_solution(17794249535125665903)
XLA Ops:
  0.6 26.2 %spod.1 = (f32[2,8,8,64]{3,2,1,0:T(8,128)}, f32[8,8]{1,0:T(8,128)}, f32[2,8,3,8,1024]{4,3,2,1,0:T(8,128)}) custom-call(f32[2,8,3,64,1024]{4,3,2,1,0:T(8,128)} %bitcast.5, f32[1,1024]{1,0:T(1,128)} %bitcast.9, f32[2,8,8,64]{3,2,1,0:T(8,128)} %bitcast.7), custom_call_target="tpu_custom_call" | custom-call | tf_op jit(solution)/shard_map/spod/pallas_call | solution.py:285
  26.8 1.5 %copy.9 = f32[2,8,64,8]{2,3,1,0:T(8,128)} copy(f32[2,8,64,8]{2,3,1,0:T(8,128)} %bitcast.8) | data formatting | bytes 65536
  28.3 1.3 %copy.10 = f32[8,8]{1,0:T(8,128)} copy(f32[8,8]{1,0:T(8,128)} %get-tuple-element.13) | data formatting | bytes 512
  29.6 2.7 %copy.11 = f32[2,8,8,3,1024]{4,2,3,1,0:T(8,128)} copy(f32[2,8,8,3,1024]{4,2,3,1,0:T(8,128)} %bitcast.6) | data formatting | bytes 3145728
where the time goes:
time: 32.5 us; the launch traced here: 32.3 us
  Pallas kernels  26.2 us (81%)
  local copies, waits for them, and re-layouts  5.47 us (17%)
  between operations  0.64 us (2%)
    pallas_call x1, Pallas kernels, per_device(): pl.pallas_call(functools.partial(spod_kernel, scaling, freqs, peers, grou...  26.2 us
    unnamed x3, local copies, waits for them, and re-layouts  5.47 us

commit v1 on v0

--- a/solution.py
+++ b/solution.py
@@ -17,21 +17,21 @@
     peers,
     groups,
     data_ref,
+    weight_hbm,
+    basis_hbm,
+    split,
+    message_ref,
+    inverse_ref,
+    buf,
     weight_ref,
     basis_ref,
-    basis_out_ref,
-    spectrum_ref,
-    modes_ref,
-    buf,
-    split,
-    stage,
+    small_sem,
     gram_out,
     gram_in,
     trace_out,
     trace_in,
     message,
     load_sem,
-    store_sem,
     gram_send,
     gram_recv,
     trace_send,
@@ -40,7 +40,7 @@
     msg_recv,
 ):
     comps, blocks, points = buf.shape[2], buf.shape[3], buf.shape[4]
-    rank = basis_ref.shape[2]
+    rank = basis_ref.shape[1]
     wide = 2 * blocks
     stride = peers // freqs
     me = lax.axis_index("pts")
@@ -54,8 +54,12 @@
     def order(i):
         return lax.rem(mine + 1 + i, freqs)
 
+    weight_load = pltpu.make_async_copy(weight_hbm, weight_ref, small_sem.at[0])
+    basis_load = pltpu.make_async_copy(basis_hbm.at[:, mine], basis_ref, small_sem.at[1])
+    weight_load.start()
     for i in range(freqs):
         load(order(i)).start()
+    basis_load.start()
 
     barrier = pltpu.get_barrier_semaphore()
     for step in range(1, peers):
@@ -67,8 +71,9 @@
             barrier, inc=1, device_id={"freq": lax.rem(row + step, groups)}, device_id_type=MESH
         )
 
+    weight_load.wait()
     root = jnp.sqrt(weight_ref[...])
-    inverse = (1.0 / blocks) / root
+    inverse_ref[...] = (1.0 / blocks) / root
     lanes = lax.broadcasted_iota(jnp.int32, (1, wide), 1)
     low_minus = jnp.where(lanes < blocks, -1.0, 1.0).astype(jnp.float32)
     high_minus = -low_minus
@@ -142,6 +147,8 @@
             device_id_type=MESH,
         )
 
+    basis_load.wait()
+
     @pl.when(is_owner)
     def _():
         def gather(step, total):
@@ -186,7 +193,7 @@
                 turned = jnp.where(which > j, turned_next, turned)
             return z
 
-        start = jnp.concatenate([basis_ref[0, mine], basis_ref[1, mine]], axis=1)
+        start = jnp.concatenate([basis_ref[0], basis_ref[1]], axis=1)
         vec = lax.fori_loop(0, ITERS, step_body, start)
         energy = jnp.sum(vec * apply(vec), axis=1, keepdims=True) * (1.0 / blocks)
         columns = lax.broadcasted_iota(jnp.int32, (rank, wide), 1)
@@ -204,7 +211,56 @@
         for step in range(1, peers):
             msg_copy(step).start()
 
-    def project(f):
+    def arrive(f):
+        pltpu.make_async_copy(message.at[f], message.at[f], msg_recv.at[f]).wait()
+
+    if stride > 1:
+
+        @pl.when(jnp.logical_not(is_owner))
+        def _():
+            arrive(mine)
+
+    def others(i, carry):
+        arrive(lax.rem(mine + i, freqs))
+        return carry
+
+    lax.fori_loop(1, freqs, others, 0)
+    message_ref[...] = message[...]
+
+    def finish(i, carry):
+        gram_copy(order(i)).wait_send()
+        return carry
+
+    lax.fori_loop(0, freqs - 1, finish, 0)
+    if stride > 1:
+
+        @pl.when(jnp.logical_not(is_owner))
+        def _():
+            gram_copy(mine).wait_send()
+
+    @pl.when(is_owner)
+    def _():
+        for step in range(1, groups):
+            trace_copy(step).wait_send()
+        for step in range(1, peers):
+            msg_copy(step).wait_send()
+
+
+def project_kernel(
+    count, inverse_ref, split, message, basis_out_ref, spectrum_ref, modes_ref, stage, store_sem
+):
+    freqs, comps, depth, points = split.shape
+    wide = depth // 2
+    blocks = wide // 2
+    rank = spectrum_ref.shape[1]
+    inverse = inverse_ref[...]
+    lanes = lax.broadcasted_iota(jnp.int32, (1, wide), 1)
+    high_minus = jnp.where(lanes < blocks, 1.0, -1.0).astype(jnp.float32)
+
+    def store(f):
+        return pltpu.make_async_copy(stage.at[f], modes_ref.at[:, f], store_sem.at[f])
+
+    def project(f, carry):
         vec = message[f, 0:rank]
         left = jnp.concatenate([high_minus * vec, pltpu.roll(vec, blocks, 1)], axis=0)
         high = left.astype(jnp.bfloat16)
@@ -217,58 +273,19 @@
             out = (out[: 2 * rank] + out[2 * rank :]) * inverse
             stage[f, 0, c] = out[:rank]
             stage[f, 1, c] = out[rank:]
+        store(f).start()
         basis_out_ref[0, f] = vec[:, :blocks]
         basis_out_ref[1, f] = pltpu.roll(vec, blocks, 1)[:, :blocks]
-        store(f).start()
-
-    def store(f):
-        return pltpu.make_async_copy(stage.at[f], modes_ref.at[:, f], store_sem.at[f])
-
-    def arrive(f):
-        pltpu.make_async_copy(message.at[f], message.at[f], msg_recv.at[f]).wait()
-
-    if stride > 1:
-
-        @pl.when(jnp.logical_not(is_owner))
-        def _():
-            arrive(mine)
-
-    project(mine)
-
-    def others(i, carry):
-        f = lax.rem(mine + freqs - i, freqs)
-        arrive(f)
-        project(f)
         return carry
 
-    lax.fori_loop(1, freqs, others, 0)
+    lax.fori_loop(0, freqs, project, 0)
 
     energies = []
     overall = jnp.zeros((1, wide), jnp.float32)
     for f in range(freqs):
         energies.append(message[f, rank : rank + 1])
         overall = overall + message[f, rank + 1 : rank + 2]
-    count = freqs * groups * blocks
     spectrum_ref[...] = (jnp.concatenate(energies, axis=0) * count / overall)[:, :rank]
-
-    def finish(i, carry):
-        gram_copy(order(i)).wait_send()
-        return carry
-
-    lax.fori_loop(0, freqs - 1, finish, 0)
-    if stride > 1:
-
-        @pl.when(jnp.logical_not(is_owner))
-        def _():
-            gram_copy(mine).wait_send()
-
-    @pl.when(is_owner)
-    def _():
-        for step in range(1, groups):
-            trace_copy(step).wait_send()
-        for step in range(1, peers):
-            msg_copy(step).wait_send()
-
     for f in range(freqs):
         store(f).wait()
 
@@ -282,25 +299,28 @@
     vmem = pl.BlockSpec(memory_space=pltpu.VMEM)
     anywhere = pl.BlockSpec(memory_space=pl.ANY)
     f32 = jnp.float32
-    basis_t, spectrum, modes_t = pl.pallas_call(
+    weight = quad_weight.reshape(1, points)
+    hbm = pl.BlockSpec(memory_space=pltpu.HBM)
+    in_hbm = functools.partial(pltpu.with_memory_space_constraint, memory_space=pltpu.HBM)
+    split, message, inverse = pl.pallas_call(
         functools.partial(spod_kernel, scaling, freqs, peers, groups),
         out_shape=(
-            jax.ShapeDtypeStruct((2, freqs, rank, blocks), f32),
-            jax.ShapeDtypeStruct((freqs, rank), f32),
-            jax.ShapeDtypeStruct((2, freqs, comps, rank, points), f32),
+            pltpu.VMEM((freqs, comps, 2 * wide, points), jnp.bfloat16),
+            pltpu.VMEM((freqs, rank + 8, wide), f32),
+            pltpu.VMEM((1, points), f32),
         ),
-        in_specs=[anywhere, vmem, vmem],
-        out_specs=(vmem, vmem, anywhere),
+        in_specs=[hbm, hbm, hbm],
+        out_specs=(vmem, vmem, vmem),
         scratch_shapes=[
             pltpu.VMEM((freqs, 2, comps, blocks, points), f32),
-            pltpu.VMEM((freqs, comps, 2 * wide, points), jnp.bfloat16),
-            pltpu.VMEM((freqs, 2, comps, rank, points), f32),
+            pltpu.VMEM((1, points), f32),
+            pltpu.VMEM((2, rank, blocks), f32),
+            pltpu.SemaphoreType.DMA((2,)),
             pltpu.VMEM((freqs, blocks, wide), f32),
             pltpu.VMEM((peers, blocks, wide), f32),
             pltpu.VMEM((8, wide), f32),
             pltpu.VMEM((groups, 8, wide), f32),
             pltpu.VMEM((freqs, rank + 8, wide), f32),
-            pltpu.SemaphoreType.DMA((freqs,)),
             pltpu.SemaphoreType.DMA((freqs,)),
             pltpu.SemaphoreType.DMA((freqs,)),
             pltpu.SemaphoreType.DMA((peers,)),
@@ -310,14 +330,30 @@
             pltpu.SemaphoreType.DMA((freqs,)),
         ],
         compiler_params=pltpu.CompilerParams(
-            collective_id=0, has_side_effects=True, vmem_limit_bytes=60 * 1024 * 1024
+            collective_id=0, has_side_effects=True, vmem_limit_bytes=40 * 1024 * 1024
         ),
         name="spod",
     )(
-        data.transpose(0, 1, 3, 2, 4),
-        quad_weight.reshape(1, points),
-        basis.transpose(0, 1, 3, 2),
+        in_hbm(data.transpose(0, 1, 3, 2, 4)),
+        in_hbm(weight),
+        in_hbm(basis.transpose(0, 1, 3, 2)),
     )
+    basis_t, spectrum, modes_t = pl.pallas_call(
+        functools.partial(project_kernel, freqs * groups * blocks),
+        out_shape=(
+            jax.ShapeDtypeStruct((2, freqs, rank, blocks), f32),
+            jax.ShapeDtypeStruct((freqs, rank), f32),
+            jax.ShapeDtypeStruct((2, freqs, comps, rank, points), f32),
+        ),
+        in_specs=[vmem, vmem, vmem],
+        out_specs=(vmem, vmem, anywhere),
+        scratch_shapes=[
+            pltpu.VMEM((freqs, 2, comps, rank, points), f32),
+            pltpu.SemaphoreType.DMA((freqs,)),
+        ],
+        compiler_params=pltpu.CompilerParams(vmem_limit_bytes=20 * 1024 * 1024),
+        name="project",
+    )(inverse, split, message)
     return (
         basis_t.transpose(0, 1, 3, 2),
         spectrum,

time: 32.5 us -> 26.8 us (0.82)
  local copies, waits for them, and re-layouts: 5.47 us -> 0 us
    unnamed x3 -> x0, local copies, waits for them, and re-layouts: 5.47 us -> none
    pallas_call x1, Pallas kernels: 26.2 us -> 21.3 us  [per_device(): pl.pallas_call(functools.partial(spod_kernel, scaling, freqs, peers, grou...]
    pallas_call x0 -> x1, Pallas kernels: none -> 4.68 us  [per_device(): pl.pallas_call(functools.partial(project_kernel, freqs * groups * blocks)...]
where the time goes in v1:
time: 26.8 us; the launch traced here: 26.7 us
  Pallas kernels  26 us (97%)
  between operations  0.64 us (2%)
    pallas_call x1, Pallas kernels, per_device(): pl.pallas_call(functools.partial(spod_kernel, scaling, freqs, peers, grou...  21.3 us
    pallas_call x1, Pallas kernels, per_device(): pl.pallas_call(functools.partial(project_kernel, freqs * groups * blocks)...  4.68 us

profile of v1, /device:TPU:0, one launch (start us, length us, event | category | flops | bytes accessed | tf_op | source)
XLA Modules:
  0.0 26.7 jit_solution(6320207480867518639)
XLA Ops:
  0.6 21.3 %spod.1 = (bf16[8,3,256,1024]{3,2,1,0:T(8,128)(2,1)S(1)}, f32[8,16,128]{2,1,0:T(8,128)S(1)}, f32[1,1024]{1,0:T(1,128)S(1)}) custom-call(f32[2,8,3,64,1024]{4,3,2,1,0:T(8,128)} %bitcast.5, f32[1,1024]{1,0:T(1,128)} %bitcast.7, f32[2,8,8,64]{3,2,1,0:T(8,128)} %bitcast.6), custom_call_target="tpu_custom_call" | custom-call | tf_op jit(solution)/shard_map/spod/pallas_call | solution.py:305
  22.0 4.7 %project.1 = (f32[2,8,8,64]{3,2,1,0:T(8,128)}, f32[8,8]{1,0:T(8,128)}, f32[2,8,3,8,1024]{4,3,2,1,0:T(8,128)}) custom-call(f32[1,1024]{1,0:T(1,128)S(1)} %get-tuple-element.9.inverse_ref, bf16[8,3,256,1024]{3,2,1,0:T(8,128)(2,1)S(1)} %get-tuple-element.10.split, f32[8,16,128]{2,1,0:T(8,128)S(1)} %get-tuple-element.11.message), custom_call_target="tpu_custom_call" | custom-call | tf_op jit(solution)/shard_map/project/pallas_call | solution.py:341

commit v2 on v1

--- a/solution.py
+++ b/solution.py
@@ -278,7 +278,7 @@
         basis_out_ref[1, f] = pltpu.roll(vec, blocks, 1)[:, :blocks]
         return carry
 
-    lax.fori_loop(0, freqs, project, 0)
+    lax.fori_loop(0, freqs, project, 0, unroll=True)
 
     energies = []
     overall = jnp.zeros((1, wide), jnp.float32)

time: 26.8 us -> 25.8 us (0.963)
  Pallas kernels: 26 us -> 25 us
    pallas_call x1, Pallas kernels: 4.68 us -> 3.66 us  [per_device(): pl.pallas_call(functools.partial(project_kernel, freqs * groups * blocks)...]
where the time goes in v2:
time: 25.8 us; the launch traced here: 25.6 us
  Pallas kernels  25 us (97%)
  between operations  0.64 us (2%)
    pallas_call x1, Pallas kernels, per_device(): pl.pallas_call(functools.partial(spod_kernel, scaling, freqs, peers, grou...  21.3 us
    pallas_call x1, Pallas kernels, per_device(): pl.pallas_call(functools.partial(project_kernel, freqs * groups * blocks)...  3.66 us

profile of v2, /device:TPU:0, one launch (start us, length us, event | category | flops | bytes accessed | tf_op | source)
XLA Modules:
  0.0 25.6 jit_solution(628831612438620626)
XLA Ops:
  0.6 21.3 %spod.1 = (bf16[8,3,256,1024]{3,2,1,0:T(8,128)(2,1)S(1)}, f32[8,16,128]{2,1,0:T(8,128)S(1)}, f32[1,1024]{1,0:T(1,128)S(1)}) custom-call(f32[2,8,3,64,1024]{4,3,2,1,0:T(8,128)} %bitcast.5, f32[1,1024]{1,0:T(1,128)} %bitcast.7, f32[2,8,8,64]{3,2,1,0:T(8,128)} %bitcast.6), custom_call_target="tpu_custom_call" | custom-call | tf_op jit(solution)/shard_map/spod/pallas_call | solution.py:305
  22.0 3.7 %project.1 = (f32[2,8,8,64]{3,2,1,0:T(8,128)}, f32[8,8]{1,0:T(8,128)}, f32[2,8,3,8,1024]{4,3,2,1,0:T(8,128)}) custom-call(f32[1,1024]{1,0:T(1,128)S(1)} %get-tuple-element.9.inverse_ref, bf16[8,3,256,1024]{3,2,1,0:T(8,128)(2,1)S(1)} %get-tuple-element.10.split, f32[8,16,128]{2,1,0:T(8,128)S(1)} %get-tuple-element.11.message), custom_call_target="tpu_custom_call" | custom-call | tf_op jit(solution)/shard_map/project/pallas_call | solution.py:341
